TPU v7x, 32 devices: a whole 2x2x4 slice. The times are simulated.
32 devices in a mesh: dp: 8 (over z, x), tensor: 4 (over y, core).
Axes of the slice: x: 2, y: 2, z: 4, core: 2. Of those that a mesh axis runs over, the one named last changes fastest.
Arguments:
- master_old: float32 [3072, 36864], P('dp', 'tensor'), may hold values from -6 to 6
- moment1_old: float32 [3072, 36864], P('dp', 'tensor'), may hold values from -4 to 4
- moment2_old: float32 [3072, 36864], P('dp', 'tensor'), may hold values from 0.0001 to 1
- grad: bfloat16 [3072, 36864], P('dp', 'tensor'), may hold values from -28 to 28
- send_slots: int32 [8, 13824], P('dp'), may hold values from 0 to 13823, each once within a row
- recv_slots: int32 [8, 13824], P('dp'), may hold values from 0 to 13823, each once within a row
Outputs:
- master_new: float32 [3072, 36864], P('dp', 'tensor')
- moment1_new: float32 [3072, 36864], P('dp', 'tensor')
- moment2_new: float32 [3072, 36864], P('dp', 'tensor')
Inputs may be any that keep to these rules, and one draw needn't show every extreme that they name: `send_slots`: each row is a permutation of 0 to 13823; entry [i, j * 1728 + q] is the old slot of the q-th block that device i of dp sends to device j. `recv_slots`: each row is a permutation of 0 to 13823; entry [j, i * 1728 + q] is the new slot on device j of the q-th block from device i.
All inputs are finite; a program needn't handle non-finite values.
Results may differ from a plain program's by a relative error of at most 0.0003.
Values sent between devices are 32-bit elements; how exact they have to be, the bound alone decides.
A program may use at most 320 MiB of HBM per device.

v0:
```python
import jax
import jax.numpy as jnp
from jax import lax
from jax.sharding import PartitionSpec as P

ROWS = 3072
FF = 36864
SEGW = 128


beta_one = 0.9
beta_two = 0.95
correct_one = 0.6513215599
correct_two = 0.4012630608
adam_eps = 1e-08
learning_rate = 0.01
weight_decay = 0.1
clip_ratio = 0.75


def swapped(block, axis, apart):
    count = lax.axis_size(axis)
    route = []
    for low in range(count):
        high = low | 1 << apart
        if high != low and high < count:
            route += [(low, high), (high, low)]
    return lax.ppermute(block, axis, route)


def per_device(master_old, moment1_old, moment2_old, grad, send_slots, recv_slots):
    rows_here, columns = master_old.shape
    half_width = columns // 2
    segments = half_width // SEGW
    blocks = rows_here * segments
    devices = lax.axis_size("dp")
    per_peer = blocks // devices
    is_even = lax.axis_index("tensor") % 2 == 0
    wide = grad.astype(jnp.float32)
    sum_squares = lax.psum(jnp.sum(wide * wide), ("dp", "tensor"))
    stacked = jnp.stack([master_old, moment1_old, moment2_old], 0)
    tiled = (
        stacked.reshape(3, rows_here, 2, segments, SEGW)
        .transpose(0, 1, 3, 2, 4)
        .reshape(3, blocks, 2, SEGW)
    )
    own_send = send_slots[0]
    own_recv = recv_slots[0]
    outgoing = jnp.take(tiled, own_send, axis=1).reshape(3, devices, per_peer, 2, SEGW)
    arrived = lax.all_to_all(outgoing, "dp", split_axis=1, concat_axis=1, tiled=True).reshape(
        3, blocks, 2, SEGW
    )
    inverse = jnp.zeros((blocks,), jnp.int32).at[own_recv].set(jnp.arange(blocks, dtype=jnp.int32))
    tiles = jnp.take(arrived, inverse, axis=1)
    first = tiles[..., 0, :]
    second = tiles[..., 1, :]
    kept = jnp.where(is_even, first, second)
    outgoing = jnp.where(is_even, second, first)
    arrived = swapped(outgoing, "tensor", 0)
    moved = jnp.where(is_even, jnp.stack([kept, arrived], -2), jnp.stack([arrived, kept], -2))
    placed = (
        moved.reshape(3, rows_here, segments, 2, SEGW)
        .transpose(0, 1, 3, 2, 4)
        .reshape(3, rows_here, columns)
    )
    new_master = placed[0]
    new_first = placed[1]
    new_second = placed[2]
    limit = clip_ratio * jnp.sqrt(jnp.float32(ROWS * FF))
    clip_scale = jnp.minimum(1.0, limit / jnp.sqrt(sum_squares + 1e-06))
    scaled = clip_scale * wide
    moment1 = beta_one * new_first + (1.0 - beta_one) * scaled
    moment2 = beta_two * new_second + (1.0 - beta_two) * scaled * scaled
    update = moment1 / correct_one / (jnp.sqrt(moment2 / correct_two) + adam_eps)
    master = new_master - learning_rate * (update + weight_decay * new_master)
    return (master, moment1, moment2)


def solution(mesh):
    in_specs = (
        P("dp", "tensor"),
        P("dp", "tensor"),
        P("dp", "tensor"),
        P("dp", "tensor"),
        P("dp", None),
        P("dp", None),
    )
    out_specs = (P("dp", "tensor"), P("dp", "tensor"), P("dp", "tensor"))
    return jax.shard_map(
        per_device, mesh=mesh, in_specs=in_specs, out_specs=out_specs, check_vma=False
    )
```

profile of v0, /device:TPU:0, one launch (start us, length us, event | category | flops | bytes accessed | tf_op | source)
XLA Modules:
  0.0 1775.3 jit_solution(4331419830557279220)
XLA Ops:
  1.6 15.1 copy.58
  16.8 15.1 copy.59
  31.8 15.1 copy.60
  46.9 30.5 %maximum_bitcast_fusion = f32[3,384,36,2,128]{1,4,2,3,0:T(8,128)} fusion(f32[1,384,2,36,128]{1,4,3,2,0:T(8,128)} %bitcast.41, f32[1,384,2,36,128]{1,4,3,2,0:T(8,128)} %bitcast.40, f32[1,384,2,36,128]{1,4,3,2,0:T(8,128)} %bitcast.39), kind=kLoop, calls=%fused_computation.3 | loop fusion | flops 21233664 | bytes 84934656 | tf_op jit(solution)/shard_map/transpose | solution.py:44
  77.4 62.2 %copy.61 = f32[3,384,36,2,128]{4,3,2,1,0:T(2,128)} copy(f32[3,384,36,2,128]{1,4,2,3,0:T(8,128)} %maximum_bitcast_fusion) | data formatting | bytes 84934656 | tf_op jit(solution)/shard_map/transpose | solution.py:44
  139.6 79.0 %gather_fusion = f32[13824,3,2,128]{3,2,1,0:T(2,128)} fusion(f32[3,13824,2,128]{3,2,1,0:T(2,128)} %bitcast.36, s32[14336]{0:T(1024)S(1)} %pad_clamp_fusion.1), kind=kCustom, calls=%fused_computation.clone | custom fusion | bytes 84989952 | tf_op jit(solution)/shard_map/jit(_take)/gather | solution.py:49
  218.6 51.9 %broadcast_select_fusion = f32[13824,3,2,128]{3,2,1,0:T(2,128)} fusion(f32[13824,3,2,128]{3,2,1,0:T(2,128)} %gather_fusion, pred[13824]{0:T(1024)(128)(4,1)S(1)} %compare_and_fusion.1), kind=kLoop, calls=%fused_computation.7 | loop fusion | flops 10616832 | bytes 84948480 | tf_op jit(solution)/shard_map/jit(_take)/select_n | solution.py:49
  270.5 28.6 %copy.62 = f32[3,8,1728,2,128]{4,3,2,0,1:T(2,128)} copy(f32[3,8,1728,2,128]{4,3,0,2,1:T(2,128)} %bitcast.35) | data formatting | bytes 84934656 | tf_op jit(solution)/shard_map/reshape | solution.py:49
  299.1 8.0 all-to-all-start
  307.3 51.2 %scatter_custom_fusion = s32[13824]{0:T(1024)S(1)} fusion(s32[13824]{0:T(1024)S(1)} %fusion.7, s32[13824]{0:T(1024)S(1)} %iota.3, s32[]{:T(128)} %constant.26.clone.1), kind=kCustom, calls=%fused_computation.32 | custom fusion | bytes 55300 | tf_op jit(solution)/shard_map/scatter | solution.py:53
  358.6 863.7 %all-to-all-done = f32[3,8,1728,2,128]{4,3,2,0,1:T(2,128)} async-done(((f32[3,8,1728,2,128]{4,3,2,0,1:T(2,128)}), f32[3,8,1728,2,128]{4,3,2,0,1:T(2,128)}, u32[]{:S(2)}, u32[]{:S(2)}) %all-to-all-start) | async-done | bytes 42467360 | tf_op jit(solution)/shard_map/all_to_all | solution.py:50
  1222.4 28.1 %copy.63 = f32[3,8,1728,2,128]{4,3,2,1,0:T(2,128)} copy(f32[3,8,1728,2,128]{4,3,2,0,1:T(2,128)} %all-to-all-done) | data formatting | bytes 84934656 | tf_op jit(solution)/shard_map/all_to_all | solution.py:50
  1250.5 79.0 %gather_fusion.1 = f32[13824,3,2,128]{3,2,1,0:T(2,128)} fusion(f32[3,13824,2,128]{3,2,1,0:T(2,128)} %bitcast.37, s32[14336]{0:T(1024)S(1)} %pad_clamp_fusion), kind=kCustom, calls=%fused_computation.1.clone | custom fusion | bytes 84989952 | tf_op jit(solution)/shard_map/jit(_take)/gather | solution.py:54
  1329.5 51.9 %select_bitcast_fusion = f32[3,13824,2,128]{3,2,0,1:T(2,128)} fusion(f32[13824,3,2,128]{3,2,1,0:T(2,128)} %gather_fusion.1, pred[13824]{0:T(1024)(128)(4,1)S(1)} %compare_and_fusion), kind=kLoop, calls=%fused_computation.6 | loop fusion | flops 10616832 | bytes 84948480 | tf_op jit(solution)/shard_map/jit(_take)/select_n | solution.py:54
  1381.4 49.3 %broadcast_select_fusion.2 = (f32[3,13824,1,128]{3,2,0,1:T(1,128)}, f32[3,13824,1,128]{3,2,0,1:T(1,128)}) fusion(pred[]{:T(512)S(6)} %eq.5, f32[3,13824,2,128]{3,2,0,1:T(2,128)} %select_bitcast_fusion), kind=kLoop, calls=%fused_computation.9 | loop fusion | flops 10616832 | bytes 84934656 | tf_op jit(solution)/shard_map/jit(_where)/select_n | solution.py:57
  1430.7 17.8 %copy.78 = f32[3,13824,1,128]{3,1,0,2:T(8,128)} copy(f32[3,13824,1,128]{3,2,0,1:T(1,128)} %get-tuple-element.23) | data formatting | bytes 42467328 | tf_op jit(solution)/shard_map/jit(_where)/select_n | solution.py:58
  1448.5 10.3 copy.72
  1458.8 6.4 fusion.3
  1465.2 48.1 %psum.7 = f32[]{:T(128)} all-reduce(f32[]{:T(128)} %fusion.3), channel_id=1, replica_groups=mesh['dp'=8,'tensor'=4] {'dp','tensor'}, use_global_device_ids=true, to_apply=%region_2.4 | all-reduce | flops 1 | bytes 8 | tf_op jit(solution)/shard_map/psum | solution.py:40
  1513.9 17.6 copy.64
  1531.5 7.9 copy.66
  1539.4 23.4 %stack.31 = f32[3,384,36,1,128]{4,2,1,0,3:T(8,128)} reshape(f32[3,13824,128]{2,1,0:T(8,128)} %collective-permute-done) | data formatting | bytes 42467328 | tf_op jit(solution)/shard_map/stack | solution.py:60
  1562.7 18.7 %copy.67 = f32[3,384,36,1,128]{4,1,2,3,0:T(8,128)} copy(f32[3,384,36,1,128]{4,2,1,0,3:T(8,128)} %stack.31) | data formatting | bytes 42467328 | tf_op jit(solution)/shard_map/stack | solution.py:60
  1581.5 42.2 %fusion = f32[3,384,2,36,128]{4,1,3,2,0:T(8,128)} fusion(f32[3,384,36,1,128]{4,1,2,3,0:T(8,128)} %copy.67, f32[3,384,36,1,128]{4,1,2,3,0:T(8,128)} %copy.66, pred[]{:T(512)S(6)} %eq.5), kind=kLoop, calls=%fused_computation.5 | loop fusion | flops 31850496 | bytes 84934656 | tf_op jit(solution)/shard_map/transpose | solution.py:63
  1623.7 28.8 %slice_multiply_fusion = (f32[1,384,2,36,128]{4,1,3,2,0:T(8,128)}, f32[1,384,2,36,128]{4,1,3,2,0:T(8,128)}, f32[1,384,2,36,128]{4,1,3,2,0:T(8,128)}) fusion(f32[3,384,2,36,128]{4,1,3,2,0:T(8,128)} %fusion), kind=kLoop, calls=%fused_computation.18 | loop fusion | flops 7077888 | bytes 84934656 | tf_op jit(solution)/shard_map/mul | solution.py:73
  1652.5 15.1 copy.70
  1667.7 15.1 copy.71
  1682.8 15.1 copy.73
  1697.9 32.1 %bitcast_subtract_fusion = (f32[384,9216]{0,1:T(8,128)}, f32[384,9216]{0,1:T(8,128)}, f32[384,9216]{0,1:T(8,128)}) fusion(f32[1,384,2,36,128]{1,4,3,2,0:T(8,128)} %copy.70, bf16[384,9216]{0,1:T(8,128)(2,1)} %copy.72, f32[]{:T(128)S(6)} %min_shard_map.3, f32[1,384,2,36,128]{1,4,3,2,0:T(8,128)} %copy.71, f32[1,384,2,36,128]{1,4,3,2,0:T(8,128)} %copy.73), kind=kLoop, calls=%fused_computation.20 | loop fusion | flops 53084160 | bytes 92012544 | tf_op jit(solution)/shard_map/sub | solution.py:75
  1730.0 15.1 copy.74
  1745.1 15.1 copy.75
  1760.2 15.1 copy.76
  (13 shorter events, 1.2 us)
Async XLA Ops:
  299.1 8.0 copy-start
  299.1 923.2 %all-to-all-start = ((f32[3,8,1728,2,128]{4,3,2,0,1:T(2,128)}), f32[3,8,1728,2,128]{4,3,2,0,1:T(2,128)}, u32[]{:S(2)}, u32[]{:S(2)}) async-start(f32[3,8,1728,2,128]{4,3,2,0,1:T(2,128)} %copy.62), calls=%async_computation | async-start | bytes 84934656 | tf_op jit(solution)/shard_map/all_to_all | solution.py:50
  1448.5 90.8 %collective-permute-start = (f32[3,13824,128]{2,1,0:T(8,128)}, f32[3,13824,128]{2,1,0:T(8,128)}, u32[]{:S(2)}, u32[]{:S(2)}) collective-permute-start(f32[3,13824,128]{2,1,0:T(8,128)} %bitcast.34), channel_id=1, source_target_pairs={{0,1},{1,0},{2,3},{3,2},{4,5},{5,4},{6,7},{7,6},{8,9},{9,8},{10,11... | collective-permute-start | bytes 63701000 | tf_op jit(solution)/shard_map/ppermute | solution.py:28
where the time goes:
time: 1790 us; the launch traced here: 1780 us
  waiting for transfers between devices  864 us (48%)
  local copies, waits for them, and re-layouts  560 us (31%)
  other arithmetic  294 us (16%)
  blocking collectives  48.1 us (3%)
    all_to_all x1, waiting for transfers between devices, per_device(): lax.all_to_all(outgoing, 'dp', split_axis=1, concat_axis=1, tiled=True)  864 us
    unnamed x9, local copies, waits for them, and re-layouts  101 us
    gather x1, local copies, waits for them, and re-layouts, per_device(): jnp.take(tiled, own_send, axis=1).reshape(3, devices, per_peer, 2, SEGW)  79 us
    gather x1, local copies, waits for them, and re-layouts, per_device(): tiles = jnp.take(arrived, inverse, axis=1)  79 us
    transpose x1, local copies, waits for them, and re-layouts, per_device(): tiled = stacked.reshape(3, rows_here, 2, segments, SEGW).transpose(0, 1,...  62.2 us
    select_n x2, other arithmetic, per_device(): tiles = jnp.take(arrived, inverse, axis=1)  51.9 us
    select_n x2, other arithmetic, per_device(): jnp.take(tiled, own_send, axis=1).reshape(3, devices, per_peer, 2, SEGW)  51.9 us
    scatter x1, local copies, waits for them, and re-layouts, per_device(): jnp.zeros((blocks,), jnp.int32).at[own_recv]  51.2 us
  transfers between devices with their start and end apart: 2, of which 1 were waited for; matrix products, arithmetic and copies ran while one was open for 5% of the time, Pallas kernels for 0%

commit v1 on v0

v1 whole, which is shorter than its diff:
```python
import jax
import jax.numpy as jnp
from jax import lax
from jax.experimental import pallas as pl
from jax.experimental.pallas import tpu as pltpu
from jax.sharding import PartitionSpec as P

ROWS = 3072
FF = 36864
SEGW = 128


beta_one = 0.9
beta_two = 0.95
correct_one = 0.6513215599
correct_two = 0.4012630608
adam_eps = 1e-08
learning_rate = 0.01
weight_decay = 0.1
clip_ratio = 0.75


def swapped(block, axis, apart):
    count = lax.axis_size(axis)
    route = []
    for low in range(count):
        high = low | 1 << apart
        if high != low and high < count:
            route += [(low, high), (high, low)]
    return lax.ppermute(block, axis, route)


VMEM_LIMIT = 60 * 1024 * 1024
UNROLL = 16


def tile_rows(matrix):
    rows, columns = matrix.shape
    return (
        matrix.reshape(rows // 8, 8, columns // SEGW, SEGW)
        .transpose(0, 2, 1, 3)
        .reshape(rows * columns // SEGW, SEGW)
    )


def from_tile_rows(lines, rows, columns):
    return (
        lines.reshape(rows // 8, columns // SEGW, 8, SEGW)
        .transpose(0, 2, 1, 3)
        .reshape(rows, columns)
    )


def line_of(slots, segments):
    row = slots // segments
    segment = slots % segments
    return (row // 8) * (2 * segments * 8) + segment * 8 + row % 8


def chunk_of(blocks):
    chunk = blocks
    for parts in (2, 4, 8):
        if blocks % (parts * UNROLL) == 0 or blocks % (parts * 8) == 0:
            chunk = blocks // parts
    return chunk


def step_of(chunk):
    return UNROLL if chunk % UNROLL == 0 else 8


def gather_kernel(lines_ref, apart_ref, x_ref, keep_ref, send_ref):
    chunk = keep_ref.shape[0]
    base = pl.program_id(0) * chunk
    keep_at = apart_ref[0]
    send_at = apart_ref[1]
    step = step_of(chunk)

    def body(i, carry):
        start = pl.multiple_of(i * step, 8)
        for k in range(step):
            line = lines_ref[base + start + k]
            keep_ref[pl.ds(start + k, 1), :] = x_ref[pl.ds(line + keep_at, 1), :]
            send_ref[pl.ds(start + k, 1), :] = x_ref[pl.ds(line + send_at, 1), :]
        return carry

    lax.fori_loop(0, chunk // step, body, 0)


def scatter_kernel(lines_ref, apart_ref, keep_ref, got_ref, out_ref):
    chunk = keep_ref.shape[0]
    base = pl.program_id(0) * chunk
    keep_at = apart_ref[0]
    got_at = apart_ref[1]
    step = step_of(chunk)

    def body(i, carry):
        start = pl.multiple_of(i * step, 8)
        for k in range(step):
            line = lines_ref[base + start + k]
            out_ref[pl.ds(line + keep_at, 1), :] = keep_ref[pl.ds(start + k, 1), :]
            out_ref[pl.ds(line + got_at, 1), :] = got_ref[pl.ds(start + k, 1), :]
        return carry

    lax.fori_loop(0, chunk // step, body, 0)


def move_call(kernel, blocks, gathering):
    chunk = chunk_of(blocks)
    whole = pl.BlockSpec((2 * blocks, SEGW), lambda i, *_: (0, 0))
    piece = pl.BlockSpec((chunk, SEGW), lambda i, *_: (i, 0))
    full = jax.ShapeDtypeStruct((2 * blocks, SEGW), jnp.float32)
    half = jax.ShapeDtypeStruct((blocks, SEGW), jnp.float32)
    return pl.pallas_call(
        kernel,
        grid_spec=pltpu.PrefetchScalarGridSpec(
            num_scalar_prefetch=2,
            grid=(blocks // chunk,),
            in_specs=[whole] if gathering else [piece, piece],
            out_specs=[piece, piece] if gathering else whole,
        ),
        out_shape=[half, half] if gathering else full,
        compiler_params=pltpu.CompilerParams(
            dimension_semantics=("arbitrary",), vmem_limit_bytes=VMEM_LIMIT
        ),
        cost_estimate=pl.CostEstimate(
            flops=0, bytes_accessed=16 * blocks * SEGW, transcendentals=0
        ),
    )


def per_device(master_old, moment1_old, moment2_old, grad, send_slots, recv_slots):
    rows_here, columns = master_old.shape
    segments = columns // 2 // SEGW
    blocks = rows_here * segments
    parity = lax.axis_index("tensor") % 2
    apart = jnp.stack([parity, 1 - parity]).astype(jnp.int32) * (segments * 8)
    send_lines = line_of(send_slots[0], segments)
    recv_lines = line_of(recv_slots[0], segments)
    gather = move_call(gather_kernel, blocks, True)
    scatter = move_call(scatter_kernel, blocks, False)

    def moved(matrix):
        keep, send = gather(send_lines, apart, tile_rows(matrix))
        got = swapped(send, "tensor", 0)
        keep = lax.all_to_all(keep, "dp", split_axis=0, concat_axis=0, tiled=True)
        got = lax.all_to_all(got, "dp", split_axis=0, concat_axis=0, tiled=True)
        return from_tile_rows(scatter(recv_lines, apart, keep, got), rows_here, columns)

    wide = grad.astype(jnp.float32)
    new_first = moved(moment1_old)
    new_second = moved(moment2_old)
    new_master = moved(master_old)
    sum_squares = lax.psum(jnp.sum(wide * wide), ("dp", "tensor"))
    limit = clip_ratio * jnp.sqrt(jnp.float32(ROWS * FF))
    clip_scale = jnp.minimum(1.0, limit / jnp.sqrt(sum_squares + 1e-06))
    scaled = clip_scale * wide
    moment1 = beta_one * new_first + (1.0 - beta_one) * scaled
    moment2 = beta_two * new_second + (1.0 - beta_two) * scaled * scaled
    update = moment1 / correct_one / (jnp.sqrt(moment2 / correct_two) + adam_eps)
    master = new_master - learning_rate * (update + weight_decay * new_master)
    return (master, moment1, moment2)


def solution(mesh):
    in_specs = (
        P("dp", "tensor"),
        P("dp", "tensor"),
        P("dp", "tensor"),
        P("dp", "tensor"),
        P("dp", None),
        P("dp", None),
    )
    out_specs = (P("dp", "tensor"), P("dp", "tensor"), P("dp", "tensor"))
    return jax.shard_map(
        per_device, mesh=mesh, in_specs=in_specs, out_specs=out_specs, check_vma=False
    )
```

time: 1790 us -> 1200 us (0.67)
  local copies, waits for them, and re-layouts: 560 us -> 3.18 us
  Pallas kernels: 0 us -> 264 us
  other arithmetic: 294 us -> 60.8 us
  waiting for transfers between devices: 864 us -> 666 us
  blocking collectives: 48.1 us -> 167 us
  starting transfers between devices: 7.98 us -> 32.1 us
    pallas_call x0 -> x6, Pallas kernels: none -> 264 us  [the longest x3 134 us: moved(): scatter(recv_lines, apart, keep, got)]
    all_to_all x1 -> x6, waiting for transfers between devices: 864 us -> 642 us  [the longest x3 388 us: moved(): got = lax.all_to_all(got, 'dp', split_axis=0, concat_axis=0, tiled=True)]
    gather x2 -> x0, local copies, waits for them, and re-layouts: 158 us -> none  [the longest x1 79 us: per_device(): jnp.take(tiled, own_send, axis=1).reshape(3, devices, per_peer, 2, SEGW)]
    select_n x6 -> x0, other arithmetic: 153 us -> none  [the longest x2 51.9 us: per_device(): tiles = jnp.take(arrived, inverse, axis=1)]
    psum x1, blocking collectives: 48.1 us -> 167 us  [per_device(): sum_squares = lax.psum(jnp.sum(wide * wide), ('dp', 'tensor'))]
    unnamed x9 -> x4, local copies, waits for them, and re-layouts: 101 us -> 3.18 us
    transpose x2 -> x0, other arithmetic: 72.7 us -> none  [the longest x1 42.2 us: per_device(): placed = moved.reshape(3, rows_here, segments, 2, SEGW).transpose(0, 1, 3...]
    transpose x1 -> x0, local copies, waits for them, and re-layouts: 62.2 us -> none  [per_device(): tiled = stacked.reshape(3, rows_here, 2, segments, SEGW).transpose(0, 1,...]
  transfers between devices with their start and end apart: 2 -> 9, of which waited for: 1 -> 7; matrix products, arithmetic and copies ran while one was open for 5% -> 2% of each run, Pallas kernels for 0% -> 15%
where the time goes in v1:
time: 1200 us; the launch traced here: 1190 us
  waiting for transfers between devices  666 us (56%)
  Pallas kernels  264 us (22%)
  blocking collectives  167 us (14%)
  other arithmetic  60.8 us (5%)
  starting transfers between devices  32.1 us (3%)
    all_to_all x3, waiting for transfers between devices, moved(): got = lax.all_to_all(got, 'dp', split_axis=0, concat_axis=0, tiled=True)  388 us
    all_to_all x3, waiting for transfers between devices, moved(): keep = lax.all_to_all(keep, 'dp', split_axis=0, concat_axis=0, tiled=True)  255 us
    psum x1, blocking collectives, per_device(): sum_squares = lax.psum(jnp.sum(wide * wide), ('dp', 'tensor'))  167 us
    pallas_call x3, Pallas kernels, moved(): scatter(recv_lines, apart, keep, got)  134 us
    pallas_call x3, Pallas kernels, moved(): keep, send = gather(send_lines, apart, tile_rows(matrix))  129 us
    sub x1, other arithmetic, per_device(): master = new_master - learning_rate * (update + weight_decay * new_master)  32.1 us
  transfers between devices with their start and end apart: 9, of which 7 were waited for; matrix products, arithmetic and copies ran while one was open for 2% of the time, Pallas kernels for 15%

profile of v1, /device:TPU:0, one launch (start us, length us, event | category | flops | bytes accessed | tf_op | source)
XLA Modules:
  0.0 1193.7 jit_solution(17483994617141911085)
XLA Ops:
  0.6 1.0 compare_reduce_fusion
  1.7 1.2 divide_reduce_fusion
  2.9 0.6 add_multiply_fusion.apart_ref
  3.5 0.7 fusion.10.lines_ref
  4.2 43.0 %shard_map.89 = (f32[13824,128]{1,0:T(8,128)}, f32[13824,128]{1,0:T(8,128)}) custom-call(s32[13824]{0:T(1024)} %fusion.10.lines_ref, s32[2]{0:T(128)} %add_multiply_fusion.apart_ref, f32[27648,128]{1,0:T(8,128)} %bitcast.47), custom_call_target="tpu_custom_call" | custom-call | bytes 28311552 | tf_op jit(solution)/shard_map/pallas_call | solution.py:144
  47.3 7.3 all-to-all-start.4
  54.6 43.0 %shard_map.87 = (f32[13824,128]{1,0:T(8,128)}, f32[13824,128]{1,0:T(8,128)}) custom-call(s32[13824]{0:T(1024)} %fusion.10.lines_ref, s32[2]{0:T(128)} %add_multiply_fusion.apart_ref, f32[27648,128]{1,0:T(8,128)} %bitcast.48), custom_call_target="tpu_custom_call" | custom-call | bytes 28311552 | tf_op jit(solution)/shard_map/pallas_call | solution.py:144
  97.6 112.1 %all-to-all-done.4 = f32[8,1728,128]{2,1,0:T(8,128)} async-done(((f32[8,1728,128]{2,1,0:T(8,128)}), f32[8,1728,128]{2,1,0:T(8,128)}, u32[]{:S(2)}, u32[]{:S(2)}) %all-to-all-start.4) | async-done | bytes 7077920 | tf_op jit(solution)/shard_map/all_to_all | solution.py:146
  209.6 4.8 all-to-all-start.2
  214.6 11.6 collective-permute-done.2
  226.2 142.5 %all-to-all-done.2 = f32[8,1728,128]{2,1,0:T(8,128)} async-done(((f32[8,1728,128]{2,1,0:T(8,128)}), f32[8,1728,128]{2,1,0:T(8,128)}, u32[]{:S(2)}, u32[]{:S(2)}) %all-to-all-start.2) | async-done | bytes 7077920 | tf_op jit(solution)/shard_map/all_to_all | solution.py:146
  368.6 4.8 all-to-all-start.5
  373.5 11.6 collective-permute-done.1
  385.2 142.3 %all-to-all-done.5 = f32[8,1728,128]{2,1,0:T(8,128)} async-done(((f32[8,1728,128]{2,1,0:T(8,128)}), f32[8,1728,128]{2,1,0:T(8,128)}, u32[]{:S(2)}, u32[]{:S(2)}) %all-to-all-start.5) | async-done | bytes 7077920 | tf_op jit(solution)/shard_map/all_to_all | solution.py:147
  527.5 4.8 all-to-all-start.3
  532.3 43.1 %shard_map.85 = (f32[13824,128]{1,0:T(8,128)}, f32[13824,128]{1,0:T(8,128)}) custom-call(s32[13824]{0:T(1024)} %fusion.10.lines_ref, s32[2]{0:T(128)} %add_multiply_fusion.apart_ref, f32[27648,128]{1,0:T(8,128)} %bitcast.49), custom_call_target="tpu_custom_call" | custom-call | bytes 28311552 | tf_op jit(solution)/shard_map/pallas_call | solution.py:144
  575.4 111.1 %all-to-all-done.3 = f32[8,1728,128]{2,1,0:T(8,128)} async-done(((f32[8,1728,128]{2,1,0:T(8,128)}), f32[8,1728,128]{2,1,0:T(8,128)}, u32[]{:S(2)}, u32[]{:S(2)}) %all-to-all-start.3) | async-done | bytes 7077920 | tf_op jit(solution)/shard_map/all_to_all | solution.py:147
  686.4 4.8 all-to-all-start
  691.4 7.3 fusion.2
  698.6 167.0 %psum.7 = f32[]{:T(128)} all-reduce(f32[]{:T(128)} %fusion.2), channel_id=1, replica_groups=mesh['dp'=8,'tensor'=4] {'dp','tensor'}, use_global_device_ids=true, to_apply=%region_1.2 | all-reduce | flops 1 | bytes 8 | tf_op jit(solution)/shard_map/psum | solution.py:154
  866.3 0.2 compare_reduce_fusion.1
  866.5 0.4 divide_reduce_fusion.1
  867.0 0.7 fusion.6.lines_ref
  867.7 44.8 %shard_map.90 = f32[27648,128]{1,0:T(8,128)} custom-call(s32[13824]{0:T(1024)} %fusion.6.lines_ref, s32[2]{0:T(128)} %add_multiply_fusion.apart_ref, f32[13824,128]{1,0:T(8,128)} %bitcast.26.keep_ref, f32[13824,128]{1,0:T(8,128)} %bitcast.28.got_ref), custom_call_target="tpu_custom_call" | custom-call | bytes 28311552 | tf_op jit(solution)/shard_map/pallas_call | solution.py:148
  912.5 44.8 %shard_map.88 = f32[27648,128]{1,0:T(8,128)} custom-call(s32[13824]{0:T(1024)} %fusion.6.lines_ref, s32[2]{0:T(128)} %add_multiply_fusion.apart_ref, f32[13824,128]{1,0:T(8,128)} %bitcast.16.keep_ref, f32[13824,128]{1,0:T(8,128)} %bitcast.18.got_ref), custom_call_target="tpu_custom_call" | custom-call | bytes 28311552 | tf_op jit(solution)/shard_map/pallas_call | solution.py:148
  957.3 5.3 all-to-all-start.1
  962.6 11.0 broadcast_multiply_fusion
  973.7 3.2 copy-done
  976.8 5.5 broadcast_multiply_fusion.1
  982.3 134.5 %all-to-all-done.1 = f32[8,1728,128]{2,1,0:T(8,128)} async-done(((f32[8,1728,128]{2,1,0:T(8,128)}), f32[8,1728,128]{2,1,0:T(8,128)}, u32[]{:S(2)}, u32[]{:S(2)}) %all-to-all-start.1) | async-done | bytes 7077920 | tf_op jit(solution)/shard_map/all_to_all | solution.py:147
  1116.8 44.8 %shard_map.86 = f32[27648,128]{1,0:T(8,128)} custom-call(s32[13824]{0:T(1024)} %fusion.6.lines_ref, s32[2]{0:T(128)} %add_multiply_fusion.apart_ref, f32[13824,128]{1,0:T(8,128)} %bitcast.6.keep_ref, f32[13824,128]{1,0:T(8,128)} %bitcast.8.got_ref), custom_call_target="tpu_custom_call" | custom-call | bytes 28311552 | tf_op jit(solution)/shard_map/pallas_call | solution.py:148
  1161.6 32.1 %multiply_subtract_fusion = (f32[384,9216]{1,0:T(8,128)}, f32[384,9216]{1,0:T(8,128)}, f32[384,9216]{1,0:T(8,128)}) fusion(f32[384,9216]{1,0:T(8,128)} %bitcast.46, f32[384,9216]{1,0:T(8,128)} %bitcast.45, bf16[384,9216]{1,0:T(8,128)(2,1)} %param.9, f32[]{:T(128)S(6)} %min_shard_map.3, f32[384,9216]{1,0:T(8,128)} %bitcast.44), kind=kLoop, calls=%fused_computation.7 | loop fusion | flops 53084160 | bytes 92012544 | tf_op jit(solution)/shard_map/sub | solution.py:161
  (8 shorter events, 0.2 us)
Async XLA Ops:
  47.3 162.4 %all-to-all-start.4 = ((f32[8,1728,128]{2,1,0:T(8,128)}), f32[8,1728,128]{2,1,0:T(8,128)}, u32[]{:S(2)}, u32[]{:S(2)}) async-start(f32[8,1728,128]{2,1,0:T(8,128)} %bitcast.52), calls=%async_computation.4 | async-start | bytes 14155776 | tf_op jit(solution)/shard_map/all_to_all | solution.py:146
  209.6 159.0 %all-to-all-start.2 = ((f32[8,1728,128]{2,1,0:T(8,128)}), f32[8,1728,128]{2,1,0:T(8,128)}, u32[]{:S(2)}, u32[]{:S(2)}) async-start(f32[8,1728,128]{2,1,0:T(8,128)} %bitcast.51), calls=%async_computation.2 | async-start | bytes 14155776 | tf_op jit(solution)/shard_map/all_to_all | solution.py:146
  214.5 11.7 collective-permute-start.2
  368.6 158.8 %all-to-all-start.5 = ((f32[8,1728,128]{2,1,0:T(8,128)}), f32[8,1728,128]{2,1,0:T(8,128)}, u32[]{:S(2)}, u32[]{:S(2)}) async-start(f32[8,1728,128]{2,1,0:T(8,128)} %bitcast.27), calls=%async_computation.5 | async-start | bytes 14155776 | tf_op jit(solution)/shard_map/all_to_all | solution.py:147
  373.5 11.7 collective-permute-start.1
  527.5 159.0 %all-to-all-start.3 = ((f32[8,1728,128]{2,1,0:T(8,128)}), f32[8,1728,128]{2,1,0:T(8,128)}, u32[]{:S(2)}, u32[]{:S(2)}) async-start(f32[8,1728,128]{2,1,0:T(8,128)} %bitcast.17), calls=%async_computation.3 | async-start | bytes 14155776 | tf_op jit(solution)/shard_map/all_to_all | solution.py:147
  575.4 290.9 %copy-start.1 = (s32[1,13824]{1,0:T(1,128)S(1)}, s32[1,13824]{1,0:T(1,128)}, u32[]{:S(2)}) copy-start(s32[1,13824]{1,0:T(1,128)} %param.11) | copy-start | bytes 165892
  686.4 270.9 %all-to-all-start = ((f32[8,1728,128]{2,1,0:T(8,128)}), f32[8,1728,128]{2,1,0:T(8,128)}, u32[]{:S(2)}, u32[]{:S(2)}) async-start(f32[8,1728,128]{2,1,0:T(8,128)} %bitcast.50), calls=%async_computation | async-start | bytes 14155776 | tf_op jit(solution)/shard_map/all_to_all | solution.py:146
  691.3 266.1 %collective-permute-start = (f32[13824,128]{1,0:T(8,128)}, f32[13824,128]{1,0:T(8,128)}, u32[]{:S(2)}, u32[]{:S(2)}) collective-permute-start(f32[13824,128]{1,0:T(8,128)} %get-tuple-element.10), channel_id=1, source_target_pairs={{0,1},{1,0},{2,3},{3,2},{4,5},{5,4},{6,7},{7,6},{8,9},{9,8},{10,11... | collective-permute-start | bytes 21233672 | tf_op jit(solution)/shard_map/ppermute | solution.py:30
  957.3 159.5 %all-to-all-start.1 = ((f32[8,1728,128]{2,1,0:T(8,128)}), f32[8,1728,128]{2,1,0:T(8,128)}, u32[]{:S(2)}, u32[]{:S(2)}) async-start(f32[8,1728,128]{2,1,0:T(8,128)} %bitcast.7), calls=%async_computation.1 | async-start | bytes 14155776 | tf_op jit(solution)/shard_map/all_to_all | solution.py:147
  962.6 14.2 %copy-start = (f32[27648,128]{1,0:T(8,128)S(1)}, f32[27648,128]{1,0:T(8,128)}, u32[]{:S(2)}) copy-start(f32[27648,128]{1,0:T(8,128)} %shard_map.88) | copy-start | bytes 42467332
